TPU v7x, 256 devices: a whole 4x4x8 slice. The times are simulated.
256 devices in a mesh: freq: 32 (over x, z), pts: 8 (over y, core).
Axes of the slice: x: 4, y: 4, z: 8, core: 2. Of those that a mesh axis runs over, the one named last changes fastest.
Arguments:
- snapshots: float32 [256, 5, 65536], P(None, None, ('pts', 'freq')), may hold values from -6 to 6
- weights: float32 [65536], P(('pts', 'freq')), may hold values from 0.25 to 4
- starts: int32 [3], replicated, may hold values from 0 to 128
- bins: int32 [64], replicated, may hold values from 0 to 63, each once
Outputs:
- modes: float32 [64, 2, 5, 65536], P('freq', None, None, 'pts')
- energy: float32 [64], P('freq')
All inputs are finite; a program needn't handle non-finite values.
Results may differ from a plain program's by a relative error of at most 0.00024.
Values sent between devices are 32-bit elements; how exact they have to be, the bound alone decides.
A program may use at most 64 MiB of HBM per device.

v0:
```python
import math

import jax
import jax.numpy as jnp
from jax import lax
from jax.sharding import Mesh
from jax.sharding import PartitionSpec as P

NFFT = 128
ITERS = 8
FREQ = ("freq_0", "freq_1")
PTS = ("pts_0", "pts_1")
PTS_FREQ = ("pts_0", "pts_1", "freq_0", "freq_1")


def from_everyone(value, axis):
    length = lax.axis_size(axis)
    return lax.all_to_all(
        jnp.broadcast_to(value[None], (length, *value.shape)), axis, 0, 0, tiled=True
    )


def taken_together(value, axis):
    return from_everyone(value, axis).sum(axis=0)


def by_axis(value, axes):
    far, near = axes
    return taken_together(taken_together(value, near), far)


def in_one(arrays, axis):
    ends = [0]
    for a in arrays:
        ends.append(ends[-1] + a.size)
    total = by_axis(jnp.concatenate([a.ravel() for a in arrays]), axis)
    return tuple((total[b:e].reshape(a.shape) for a, b, e in zip(arrays, ends, ends[1:])))


def dft_tables(bins, nfft):
    steps_i = jnp.arange(nfft, dtype=jnp.int32)
    steps_t = steps_i.astype(jnp.float32)
    window = 0.5 - 0.5 * jnp.cos(2.0 * math.pi * steps_t / nfft)
    scale = 1.0 / jnp.sqrt(jnp.sum(window * window))
    phase = (bins[:, None] * steps_i[None, :] % nfft).astype(jnp.float32) * (2.0 * math.pi / nfft)
    return jnp.stack([jnp.cos(phase) * window * scale, -jnp.sin(phase) * window * scale])


def gram_of(spec, wts, count):
    weighted = spec * wts
    real_part = jnp.einsum("kacvp,kbcvp->kab", weighted, spec, precision=lax.Precision.HIGHEST)
    cross = jnp.einsum(
        "kavp,kbvp->kab", weighted[:, :, 0], spec[:, :, 1], precision=lax.Precision.HIGHEST
    )
    return (real_part / count, (cross - jnp.swapaxes(cross, 1, 2)) / count)


def apply_gram(gram_re, gram_im, xr, xi):
    ur = jnp.sum(gram_re * xr[:, None, :], 2) - jnp.sum(gram_im * xi[:, None, :], 2)
    ui = jnp.sum(gram_re * xi[:, None, :], 2) + jnp.sum(gram_im * xr[:, None, :], 2)
    return (ur, ui)


def leading(gram_re, gram_im):
    xr = jnp.ones(gram_re.shape[:2], gram_re.dtype)
    xi = jnp.zeros(gram_re.shape[:2], gram_re.dtype)
    for step in range(ITERS):
        ur, ui = apply_gram(gram_re, gram_im, xr, xi)
        scale_now = jnp.sqrt(jnp.sum(ur * ur + ui * ui, 1))[:, None]
        xr, xi = (ur / scale_now, ui / scale_now)
    ur, ui = apply_gram(gram_re, gram_im, xr, xi)
    return (xr, xi, jnp.sum(xr * ur + xi * ui, 1))


def build_modes(spec, xr, xi, energy):
    hp = lax.Precision.HIGHEST
    real_part = jnp.einsum("kb,kbvp->kvp", xr, spec[:, :, 0], precision=hp) - jnp.einsum(
        "kb,kbvp->kvp", xi, spec[:, :, 1], precision=hp
    )
    imag_part = jnp.einsum("kb,kbvp->kvp", xr, spec[:, :, 1], precision=hp) + jnp.einsum(
        "kb,kbvp->kvp", xi, spec[:, :, 0], precision=hp
    )
    factor = 1.0 / jnp.sqrt(jnp.maximum(energy, 0.25))
    return jnp.stack([real_part, imag_part], 1) * factor[:, None, None, None]


def body(snapshots, weights, starts, bins):
    n_time, n_var, n_local = snapshots.shape
    n_blocks = starts.shape[0]
    centered = snapshots - jnp.mean(snapshots, 0, keepdims=True)
    flat = centered.reshape(n_time, n_var * n_local)
    segments = jnp.stack(
        [lax.dynamic_slice_in_dim(flat, starts[block], NFFT, 0) for block in range(n_blocks)]
    )
    tables = dft_tables(bins, NFFT)
    spec = jnp.einsum("ckt,btn->kbcn", tables, segments, precision=lax.Precision.HIGHEST)
    spec = spec.reshape(bins.shape[0], n_blocks, 2, n_var, n_local)
    total_points = n_local * lax.axis_size(FREQ) * lax.axis_size(PTS)
    count = float(total_points * n_var)
    gram_re, gram_im = gram_of(spec, weights, count)
    gram_re, gram_im = in_one((gram_re, gram_im), (("freq_0", "freq_1"), ("pts_0", "pts_1")))
    xr, xi, energy_all = leading(gram_re, gram_im)
    local_modes = build_modes(spec, xr, xi, energy_all)
    modes = lax.all_to_all(local_modes, FREQ, split_axis=0, concat_axis=3, tiled=True)
    per_dev = bins.shape[0] // lax.axis_size(FREQ)
    energy = lax.dynamic_slice_in_dim(energy_all, lax.axis_index(FREQ) * per_dev, per_dev, 0)
    return (modes, energy)


def solution(mesh):
    split = Mesh(mesh.devices.reshape(4, 8, 4, 2), ("freq_0", "freq_1", "pts_0", "pts_1"))
    placed = (P(None, None, PTS_FREQ), P(PTS_FREQ), P(), P())
    return jax.shard_map(
        body,
        mesh=split,
        in_specs=placed,
        out_specs=(P(FREQ, None, None, PTS), P(FREQ)),
        check_vma=False,
    )
```

profile of v0, /device:TPU:32, one launch (start us, length us, event | category | flops | bytes accessed | tf_op | source)
XLA Modules:
  0.0 114.8 jit_solution(1240332461384616292)
XLA Ops:
  0.6 1.5 %fusion.27 = (s32[1]{0:T(128)}, s32[1]{0:T(128)}, s32[1]{0:T(128)}) fusion(s32[3]{0:T(128)} %param.6), kind=kLoop, calls=%fused_computation.112 | loop fusion | bytes 24 | tf_op jit(solution)/shard_map/slice | solution.py:93
  6.1 0.7 multiply_reduce_fusion.34
  6.8 1.7 %copy.61 = f32[256,5,256]{0,2,1:T(8,128)S(1)} copy(f32[256,5,256]{2,0,1:T(8,128)} %param.4) | data formatting | bytes 2621440 | tf_op args[0]
  8.5 0.1 reduce_sum.441
  10.6 0.2 broadcast_subtract_fusion
  10.8 0.6 constant_dynamic-slice_fusion.2
  11.4 1.1 copy.62
  12.5 0.2 copy.63
  12.8 1.1 copy.64
  14.5 0.2 multiply_multiply_fusion.1
  14.7 2.9 %convolution_bitcast_fusion = f32[64,3,2,1280]{3,0,2,1:T(8,128)S(1)} fusion(f32[1,128,1280]{2,1,0:T(8,128)} %bitcast.82, f32[1,128,1280]{2,1,0:T(8,128)S(1)} %bitcast.81, f32[1,128,1280]{2,1,0:T(8,128)S(1)} %bitcast.80, f32[1,64,128]{2,1,0:T(8,128)S(1)} %get-tuple-element.86, f32[1,64,128]{2,1,0:T(8,128)S(1)} %get-tuple-element.85), kind=kOutput, calls=%fused_computation | convolution fusion | flops 755974144 | bytes 3997696 | tf_op jit(solution)/shard_map/ckt,btn->kbcn/dot_general | solution.py:96
  17.7 2.0 %reshape.510 = f32[64,3,2,5,256]{4,3,0,2,1:T(8,128)} reshape(f32[64,3,2,1280]{3,0,2,1:T(8,128)S(1)} %convolution_bitcast_fusion) | data formatting | bytes 3932160 | tf_op jit(solution)/shard_map/reshape | solution.py:97
  19.6 3.6 %broadcast_multiply_fusion = (f32[64,3,2,5,256]{4,1,3,0,2:T(4,128)S(1)}, f32[64,3,2,5,256]{4,1,3,0,2:T(4,128)S(1)}) fusion(f32[256]{0:T(256)S(1)} %copy-done.3, f32[64,3,2,5,256]{4,3,0,2,1:T(8,128)} %reshape.510), kind=kLoop, calls=%fused_computation.10 | loop fusion | flops 491520 | bytes 5899264 | tf_op jit(solution)/shard_map/mul | solution.py:50
  23.2 10.7 %fusion.6 = f32[64,3,3]{2,1,0:T(4,128)S(1)} fusion(f32[64,3,2,5,256]{4,1,3,0,2:T(4,128)S(1)} %get-tuple-element.79, f32[256]{0:T(256)S(1)} %copy-done.3), kind=kOutput, calls=%fused_computation.13 | convolution fusion | flops 18186816 | bytes 1969408 | tf_op jit(solution)/shard_map/kacvp,kbcvp->kab/dot_general | solution.py:51
  34.0 5.5 %fusion.5 = f32[64,3,3]{2,1,0:T(4,128)S(1)} fusion(f32[64,3,2,5,256]{4,1,3,0,2:T(4,128)S(1)} %get-tuple-element.78, f32[64,3,2,5,256]{4,1,3,0,2:T(4,128)S(1)} %get-tuple-element.79), kind=kOutput, calls=%fused_computation.11 | convolution fusion | flops 8847360 | bytes 2623744 | tf_op jit(solution)/shard_map/kavp,kbvp->kab/dot_general | solution.py:52
  39.5 0.5 copy.68
  40.0 0.2 reshape.512
  40.2 0.2 reshape.511
  40.5 0.1 pad_maximum_fusion
  40.6 9.7 %all_to_all.30 = f32[8,1,1152]{2,1,0:T(1,128)S(1)} all-to-all(f32[8,1,1152]{2,1,0:T(1,128)S(1)} %broadcast_in_dim.4), channel_id=1, replica_groups=mesh['freq_0'=4,'freq_1'=8,'pts_0'=4,'pts_1'=2] {'pts_0','pts_1'}, dimensions={0} | all-to-all | bytes 73728 | tf_op jit(solution)/shard_map/all_to_all | solution.py:18
  50.3 0.7 broadcast_in_dim.5
  51.1 11.2 %all-to-all-start.1 = ((f32[32,1,1152]{2,1,0:T(1,128)}), f32[32,1,1152]{2,1,0:T(1,128)S(1)}, u32[]{:S(2)}, u32[]{:S(2)}) async-start(f32[32,1,1152]{2,1,0:T(1,128)} %broadcast_in_dim.5), calls=%async_computation.1 | async-start | bytes 294912 | tf_op jit(solution)/shard_map/all_to_all | solution.py:18
  62.3 2.7 %slice_bitcast_fusion = f32[64,3,5,256]{3,2,0,1:T(8,128)} fusion(f32[64,3,2,5,256]{4,3,0,2,1:T(8,128)} %reshape.510), kind=kLoop, calls=%fused_computation.6 | loop fusion | bytes 1966080 | tf_op jit(solution)/shard_map/squeeze | solution.py:77
  64.9 7.3 %all-to-all-done.1 = f32[32,1,1152]{2,1,0:T(1,128)S(1)} async-done(((f32[32,1,1152]{2,1,0:T(1,128)}), f32[32,1,1152]{2,1,0:T(1,128)S(1)}, u32[]{:S(2)}, u32[]{:S(2)}) %all-to-all-start.1) | async-done | bytes 147488 | tf_op jit(solution)/shard_map/all_to_all | solution.py:18
  72.3 0.1 reduce_sum.444
  72.4 0.1 fusion.26
  72.4 0.2 slice.53
  72.7 0.3 slice.55
  73.0 0.3 multiply_reduce_fusion.33
  73.3 0.1 add_reduce_fusion.8
  73.4 0.1 broadcast_divide_fusion.14
  73.5 0.4 multiply_reduce_fusion.31
  73.9 0.1 add_reduce_fusion.7
  74.0 0.1 broadcast_divide_fusion.12
  74.1 0.4 multiply_reduce_fusion.27
  74.5 0.1 add_reduce_fusion.6
  74.6 0.1 broadcast_divide_fusion.10
  74.7 0.4 multiply_reduce_fusion.23
  75.1 0.1 add_reduce_fusion.5
  75.2 0.1 broadcast_divide_fusion.8
  75.3 0.4 multiply_reduce_fusion.19
  75.6 0.1 add_reduce_fusion.4
  75.8 0.1 broadcast_divide_fusion.6
  75.9 0.4 multiply_reduce_fusion.15
  76.2 0.1 add_reduce_fusion.3
  76.4 0.1 broadcast_divide_fusion.4
  76.4 0.4 multiply_reduce_fusion.11
  76.8 0.1 add_reduce_fusion.2
  76.9 0.1 broadcast_divide_fusion.2
  77.0 0.4 multiply_reduce_fusion.7
  77.4 0.1 add_reduce_fusion.1
  77.5 0.1 broadcast_divide_fusion.1
  77.6 0.3 multiply_reduce_fusion.3
  78.0 2.3 %fusion.11 = f32[64,1,5,256]{3,1,2,0:T(1,128)S(1)} fusion(f32[64,3,1,1]{1,2,3,0:T(1,128)S(1)} %bitcast.83, f32[64,3,2,5,256]{4,1,3,0,2:T(4,128)S(1)} %get-tuple-element.79), kind=kOutput, calls=%fused_computation.18 | convolution fusion | flops 2949120 | bytes 1671168 | tf_op jit(solution)/shard_map/kb,kbvp->kvp/dot_general | solution.py:80
  80.3 2.7 %fusion.9 = f32[64,1,5,256]{3,1,2,0:T(1,128)S(1)} fusion(f32[64,3,1,1]{1,2,3,0:T(1,128)S(1)} %bitcast.84, f32[64,3,5,256]{3,2,0,1:T(8,128)S(1)} %copy-done), kind=kOutput, calls=%fused_computation.16 | convolution fusion | flops 2949120 | bytes 1311488 | tf_op jit(solution)/shard_map/kb,kbvp->kvp/dot_general | solution.py:77
  83.0 2.3 %fusion.12 = f32[64,1,5,256]{3,1,2,0:T(1,128)S(1)} fusion(f32[64,3,1,1]{1,2,3,0:T(1,128)S(1)} %bitcast.85, f32[64,3,2,5,256]{4,1,3,0,2:T(4,128)S(1)} %get-tuple-element.79), kind=kOutput, calls=%fused_computation.19 | convolution fusion | flops 2949120 | bytes 1671168 | tf_op jit(solution)/shard_map/kb,kbvp->kvp/dot_general | solution.py:77
  85.2 3.0 %fusion.7 = f32[64,1,5,256]{3,1,2,0:T(1,128)S(1)} fusion(f32[64,3,1,1]{1,2,3,0:T(1,128)S(1)} %bitcast.86, f32[64,3,5,256]{3,2,0,1:T(8,128)S(1)} %copy-done), kind=kOutput, calls=%fused_computation.14 | convolution fusion | flops 2949120 | bytes 1311488 | tf_op jit(solution)/shard_map/kb,kbvp->kvp/dot_general | solution.py:80
  88.2 0.1 add_reduce_fusion
  88.5 0.1 maximum_multiply_fusion
  88.6 1.3 %copy.71 = f32[64,2,5,256]{3,1,2,0:T(2,128)} copy(f32[64,2,5,256]{3,0,2,1:T(8,128)S(1)} %maximum_multiply_fusion) | data formatting | bytes 1310720 | tf_op jit(solution)/shard_map/mul | solution.py:84
  89.9 4.3 %all-to-all-start.2 = ((f32[64,2,5,256]{3,1,2,0:T(2,128)}), f32[64,2,5,256]{3,1,2,0:T(2,128)S(1)}, u32[]{:S(2)}, u32[]{:S(2)}) async-start(f32[64,2,5,256]{3,1,2,0:T(2,128)} %copy.71), calls=%async_computation.2 | async-start | bytes 1310720 | tf_op jit(solution)/shard_map/all_to_all | solution.py:104
  94.3 0.6 dynamic_slice.15
  94.9 18.8 %all-to-all-done.2 = f32[64,2,5,256]{3,1,2,0:T(2,128)S(1)} async-done(((f32[64,2,5,256]{3,1,2,0:T(2,128)}), f32[64,2,5,256]{3,1,2,0:T(2,128)S(1)}, u32[]{:S(2)}, u32[]{:S(2)}) %all-to-all-start.2) | async-done | bytes 655392 | tf_op jit(solution)/shard_map/all_to_all | solution.py:104
  113.6 1.1 copy.87
  (26 shorter events, 0.3 us)
Async XLA Ops:
  0.6 7.9 %copy-start.1 = (f32[256,5,256]{2,0,1:T(8,128)S(1)}, f32[256,5,256]{2,0,1:T(8,128)}, u32[]{:S(2)}) copy-start(f32[256,5,256]{2,0,1:T(8,128)} %param.4) | copy-start | bytes 3932164
  11.4 3.1 %copy-start.4 = (s32[64]{0:T(128)S(1)}, s32[64]{0:T(128)}, u32[]{:S(2)}) copy-start(s32[64]{0:T(128)} %param.7) | copy-start | bytes 772
  12.5 2.2 %copy-start.2 = (f32[128,1280]{1,0:T(8,128)S(1)}, f32[128,1280]{1,0:T(8,128)}, u32[]{:S(2)}) copy-start(f32[128,1280]{1,0:T(8,128)} %copy.62) | copy-start | bytes 1966084
  17.7 2.0 %copy-start.3 = (f32[256]{0:T(256)S(1)}, f32[256]{0:T(256)}, u32[]{:S(2)}) copy-start(f32[256]{0:T(256)} %param.5) | copy-start | bytes 3076
  51.1 21.2 %all-to-all-start.1 = ((f32[32,1,1152]{2,1,0:T(1,128)}), f32[32,1,1152]{2,1,0:T(1,128)S(1)}, u32[]{:S(2)}, u32[]{:S(2)}) async-start(f32[32,1,1152]{2,1,0:T(1,128)} %broadcast_in_dim.5), calls=%async_computation.1 | async-start | bytes 294912 | tf_op jit(solution)/shard_map/all_to_all | solution.py:18
  76.3 3.9 %copy-start = (f32[64,3,5,256]{3,2,0,1:T(8,128)S(1)}, f32[64,3,5,256]{3,2,0,1:T(8,128)}, u32[]{:S(2)}) copy-start(f32[64,3,5,256]{3,2,0,1:T(8,128)} %slice_bitcast_fusion) | copy-start | bytes 2949124
  89.9 23.7 %all-to-all-start.2 = ((f32[64,2,5,256]{3,1,2,0:T(2,128)}), f32[64,2,5,256]{3,1,2,0:T(2,128)S(1)}, u32[]{:S(2)}, u32[]{:S(2)}) async-start(f32[64,2,5,256]{3,1,2,0:T(2,128)} %copy.71), calls=%async_computation.2 | async-start | bytes 1310720 | tf_op jit(solution)/shard_map/all_to_all | solution.py:104
where the time goes:
time: 115 us
  matrix products  29.4 us (26%)
  waiting for transfers between devices  26.1 us (23%)
  local copies, waits for them, and re-layouts  16.1 us (14%)
  starting transfers between devices  15.5 us (13%)
  other arithmetic  10.2 us (9%)
  blocking collectives  9.74 us (8%)
  between operations  7.66 us (7%)
    all_to_all x1, waiting for transfers between devices, body(): lax.all_to_all(local_modes, FREQ, split_axis=0, concat_axis=3, tiled=True)  18.8 us
    all_to_all x1, starting transfers between devices, from_everyone(): lax.all_to_all(jnp.broadcast_to(value[None], (length, *value.shape)), axi...  11.2 us
    dot_general x1, matrix products, gram_of(): jnp.einsum('kacvp,kbcvp->kab', weighted, spec, precision=lax.Precision.HI...  10.7 us
    all_to_all x1, blocking collectives, from_everyone(): lax.all_to_all(jnp.broadcast_to(value[None], (length, *value.shape)), axi...  9.74 us
    all_to_all x1, waiting for transfers between devices, from_everyone(): lax.all_to_all(jnp.broadcast_to(value[None], (length, *value.shape)), axi...  7.35 us
    dot_general x1, matrix products, gram_of(): jnp.einsum('kavp,kbvp->kab', weighted[:, :, 0], spec[:, :, 1], precision=...  5.51 us
    all_to_all x1, starting transfers between devices, body(): lax.all_to_all(local_modes, FREQ, split_axis=0, concat_axis=3, tiled=True)  4.33 us
    mul x1, other arithmetic, gram_of(): weighted = spec * wts  3.58 us
  transfers between devices with their start and end apart: 2, of which 2 were waited for; matrix products, arithmetic and copies ran while one was open for 3% of the time, Pallas kernels for 0%

commit v1 on v0

v1 whole, which is shorter than its diff:
```python
import functools
import math

import jax
import jax.numpy as jnp
from jax import lax
from jax.experimental import pallas as pl
from jax.experimental.pallas import tpu as pltpu
from jax.sharding import PartitionSpec as P

NFFT = 128
NB = 3
ITERS = 8
HALF = 64
PAIRS = ((0, 1), (0, 2), (1, 2))
MESH = pl.DeviceIdType.MESH


def half_angle(steps):
    h = steps.astype(jnp.float32) * (math.pi / NFFT)
    z = h * h
    s = jnp.float32(1.0 / math.factorial(13))
    for n in (11, 9, 7, 5, 3, 1):
        s = (1.0 if (n // 2) % 2 == 0 else -1.0) / math.factorial(n) + s * z
    c = jnp.float32(1.0 / math.factorial(12))
    for n in (10, 8, 6, 4, 2, 0):
        c = (1.0 if (n // 2) % 2 == 0 else -1.0) / math.factorial(n) + c * z
    return s * h, c


def split(value):
    high = value.astype(jnp.bfloat16)
    return high, (value - high.astype(jnp.float32)).astype(jnp.bfloat16)


def fill_tables(starts, bins, lhs, kf, n_time):
    shape = (kf, n_time)
    row = jnp.broadcast_to(bins[...].astype(jnp.float32), (kf, kf))
    eye = lax.broadcasted_iota(jnp.int32, (kf, kf), 0) == lax.broadcasted_iota(
        jnp.int32, (kf, kf), 1
    )
    column = jnp.sum(jnp.where(eye, row, 0.0), axis=1, keepdims=True).astype(jnp.int32)
    lane = lax.broadcasted_iota(jnp.int32, shape, 1)
    scale = 1.0 / math.sqrt(NFFT * 3 / 8)
    for block in range(NB):
        t = lane - starts[block]
        sin_w, _ = half_angle(jnp.clip(64 - jnp.abs(t - 64), 0, 64))
        window = sin_w * sin_w * scale
        window = jnp.where((t >= 0) & (t < NFFT), window, 0.0)
        sin_h, cos_h = half_angle((((column * t) + 64) & (NFFT - 1)) - 64)
        for part, table in enumerate((1.0 - 2.0 * sin_h * sin_h, -2.0 * sin_h * cos_h)):
            rows = pl.ds((2 * block + part) * kf, kf)
            high, low = split(table * window)
            lhs[rows, 0:n_time] = high
            lhs[rows, n_time : 2 * n_time] = high
            lhs[rows, 2 * n_time : 3 * n_time] = low


def eight_bins(spec, kf, octet, v, cut):
    return [
        [spec[v, pl.ds((2 * b + part) * kf + octet * 8, 8), cut] for part in range(2)]
        for b in range(NB)
    ]


def exchange(value, mine, axis, length, source, landed, sends, recvs):
    me = lax.axis_index(axis)
    source[...] = value
    landed[me] = value

    def copy(peer, slot):
        return pltpu.make_async_remote_copy(
            src_ref=source,
            dst_ref=landed.at[slot],
            send_sem=sends.at[peer],
            recv_sem=recvs.at[slot],
            device_id={axis: peer},
            device_id_type=MESH,
        )

    def send(d, carry):
        copy(lax.rem(me + length - d, length), me).start()
        return carry

    def wait(d, carry):
        peer = lax.rem(me + d, length)
        copy(peer, peer).wait_recv()
        return carry

    def drain(d, carry):
        copy(lax.rem(me + length - d, length), me).wait_send()
        return carry

    lax.fori_loop(1, length, send, 0)
    lax.fori_loop(1, length, wait, 0)
    total = landed[0]
    for peer in range(1, length):
        total += landed[peer]
    return total, lambda: lax.fori_loop(1, length, drain, 0)


def leading(total):
    other = pltpu.roll(total, HALF, 1)
    q = [(total if n % 2 == 0 else other)[n // 2 : n // 2 + 1, :] for n in range(9)]
    re = {(a, a): q[a] for a in range(NB)}
    im = {}
    for n, (a, c) in enumerate(PAIRS):
        re[a, c] = re[c, a] = q[3 + n]
        im[a, c], im[c, a] = q[6 + n], -q[6 + n]

    def apply(xr, xi):
        ur, ui = [], []
        for a in range(NB):
            r, i = re[a, a] * xr[a], re[a, a] * xi[a]
            for c in range(NB):
                if c != a:
                    r = r + (re[a, c] * xr[c] - im[a, c] * xi[c])
                    i = i + (re[a, c] * xi[c] + im[a, c] * xr[c])
            ur.append(r)
            ui.append(i)
        return ur, ui

    def step(_, x):
        ur, ui = apply(x[:NB], x[NB:])
        norm = sum(r * r + i * i for r, i in zip(ur, ui))
        scale = 1.0 / jnp.sqrt(norm)
        return tuple(r * scale for r in ur) + tuple(i * scale for i in ui)

    one = jnp.ones_like(q[0])
    x = lax.fori_loop(0, ITERS, step, (one,) * NB + (one - one,) * NB)
    ur, ui = apply(x[:NB], x[NB:])
    energy = sum(x[a] * ur[a] + x[NB + a] * ui[a] for a in range(NB))
    factor = 1.0 / jnp.sqrt(jnp.maximum(energy, 0.25))
    return [v * factor for v in x], energy


def kernel(
    sizes, snap, wts, starts, bins, rec, energy_out,
    xbuf, lhs, rhs, spec, acc, g1, g1r, g2, g2r, coef, send,
    load_sem, s1, r1, s2, r2, s3, r3,
):
    n_freq, n_pts, kf, n_var, n_time, n_local = sizes
    per_dev = kf // n_freq
    me_f, me_p = lax.axis_index("freq"), lax.axis_index("pts")

    def load(v):
        return pltpu.make_async_copy(snap.at[v], xbuf.at[v], load_sem.at[v])

    for v in range(n_var):
        load(v).start()

    barrier = pltpu.get_barrier_semaphore()

    def greet(axis, me, length):
        def one(d, carry):
            pl.semaphore_signal(
                barrier,
                inc=1,
                device_id={axis: lax.rem(me + d, length)},
                device_id_type=MESH,
            )
            return carry

        lax.fori_loop(1, length, one, 0)

    greet("freq", me_f, n_freq)
    greet("pts", me_p, n_pts)

    fill_tables(starts, bins, lhs, kf, n_time)
    acc[...] = jnp.zeros_like(acc)

    def transform(v, carry):
        load(v).wait()
        x = xbuf[v]
        x = x - jnp.sum(x, axis=0, keepdims=True) * (1.0 / n_time)
        high, low = split(x)
        rhs[0:n_time, :] = high
        rhs[n_time : 2 * n_time, :] = low
        rhs[2 * n_time : 3 * n_time, :] = high
        spec[v] = jnp.dot(lhs[...], rhs[...], preferred_element_type=jnp.float32)
        return carry

    lax.fori_loop(0, n_var, transform, 0)

    cuts = [slice(128 * n, 128 * n + 128) for n in range(n_local // 128)]

    def gram(octet, carry):
        sums = [jnp.zeros((8, 128), jnp.float32)] * 9
        for v in range(n_var):
            for cut in cuts:
                s = eight_bins(spec, kf, octet, v, cut)
                w = jnp.broadcast_to(wts[:, cut], (8, 128))
                ws = [[w * part for part in one] for one in s]
                terms = [ws[a][0] * s[a][0] + ws[a][1] * s[a][1] for a in range(NB)]
                terms += [ws[a][0] * s[c][0] + ws[a][1] * s[c][1] for a, c in PAIRS]
                terms += [ws[a][0] * s[c][1] - ws[a][1] * s[c][0] for a, c in PAIRS]
                sums = [x + y for x, y in zip(sums, terms)]
        for n in range(9):
            acc[pl.ds(n * HALF + octet * 8, 8), :] = sums[n]
        return carry

    lax.fori_loop(0, kf // 8, gram, 0)

    parts = acc[...]
    first = parts.astype(jnp.bfloat16)
    second, third = split(parts - first.astype(jnp.float32))
    by_lane = lax.dot_general(
        jnp.ones((8, 3 * 128), jnp.bfloat16),
        jnp.concatenate([first, second, third], axis=1),
        (((1,), (1,)), ((), ())),
        preferred_element_type=jnp.float32,
    )
    sublane = lax.broadcasted_iota(jnp.int32, (8, 128), 0)
    mine = jnp.zeros((8, 128), jnp.float32)
    for n in range(5):
        mine = jnp.where(sublane == n, by_lane[:, n * 128 : n * 128 + 128], mine)

    pl.semaphore_wait(barrier, n_freq + n_pts - 2)
    near, drain_near = exchange(mine, me_p, "pts", n_pts, g1, g1r, s1, r1)
    total, drain_far = exchange(near, me_f, "freq", n_freq, g2, g2r, s2, r2)
    total = total / float(n_freq * n_pts * n_local * n_var)

    coefs, energy = leading(total)
    energy_out[...] = pltpu.roll(energy, lax.rem(128 - per_dev * me_f, 128), 1)
    table = jnp.zeros((128, 128), jnp.float32)
    wide = lax.broadcasted_iota(jnp.int32, (128, 128), 0)
    for n, c in enumerate(coefs):
        table = jnp.where(wide == n, jnp.broadcast_to(c, (128, 128)), table)
    coef[...] = jnp.transpose(table)

    dests = 8 // per_dev
    rows = per_dev * n_var * 2 * len(cuts)
    stride = rows // per_dev

    def give(dest, slot):
        return pltpu.make_async_remote_copy(
            src_ref=send.at[pl.ds(dest * rows, rows), :],
            dst_ref=rec.at[pl.ds(slot * rows, rows), :],
            send_sem=s3.at[dest],
            recv_sem=r3.at[slot],
            device_id={"freq": dest},
            device_id_type=MESH,
        )

    n_oct = kf // 8

    def modes(i, carry):
        octet = lax.rem(me_f // dests + 1 + i, n_oct)
        c = coef[pl.ds(octet * 8, 8), :]
        wide = [jnp.broadcast_to(c[:, n : n + 1], (8, 128)) for n in range(2 * NB)]
        for v in range(n_var):
            for n, cut in enumerate(cuts):
                s = eight_bins(spec, kf, octet, v, cut)
                re = sum(wide[b] * s[b][0] - wide[NB + b] * s[b][1] for b in range(NB))
                im = sum(wide[b] * s[b][1] + wide[NB + b] * s[b][0] for b in range(NB))
                for part, value in enumerate((re, im)):
                    at = octet * (8 * stride) + (v * len(cuts) + n) * 2 + part
                    send[pl.ds(at, 8, stride=stride), :] = value
        for d in range(dests):
            dest = octet * dests + d

            @pl.when(dest != me_f)
            def _():
                give(dest, me_f).start()

            @pl.when(dest == me_f)
            def _():
                rec[pl.ds(me_f * rows, rows), :] = send[pl.ds(me_f * rows, rows), :]

        return carry

    lax.fori_loop(0, n_oct, modes, 0)

    def take(d, carry):
        peer = lax.rem(me_f + d, n_freq)
        give(peer, peer).wait_recv()
        return carry

    def sent(d, carry):
        give(lax.rem(me_f + d, n_freq), me_f).wait_send()
        return carry

    lax.fori_loop(1, n_freq, take, 0)
    lax.fori_loop(1, n_freq, sent, 0)
    drain_near()
    drain_far()


def body(n_freq, n_pts, snapshots, weights, starts, bins):
    n_time, n_var, n_local = snapshots.shape
    kf = bins.shape[0]
    per_dev = kf // n_freq
    tiles = n_local // 128
    rows = kf * n_var * 2 * tiles
    sizes = (n_freq, n_pts, kf, n_var, n_time, n_local)
    vmem = pl.BlockSpec(memory_space=pltpu.VMEM)
    dma = pltpu.SemaphoreType.DMA
    rec, energy = pl.pallas_call(
        functools.partial(kernel, sizes),
        out_shape=(
            jax.ShapeDtypeStruct((rows, 128), jnp.float32),
            jax.ShapeDtypeStruct((1, 128), jnp.float32),
        ),
        in_specs=[
            pl.BlockSpec(memory_space=pl.ANY),
            vmem,
            pl.BlockSpec(memory_space=pltpu.SMEM),
            vmem,
        ],
        out_specs=(vmem, vmem),
        scratch_shapes=[
            pltpu.VMEM((n_var, n_time, n_local), jnp.float32),
            pltpu.VMEM((2 * NB * kf, 3 * n_time), jnp.bfloat16),
            pltpu.VMEM((3 * n_time, n_local), jnp.bfloat16),
            pltpu.VMEM((n_var, 2 * NB * kf, n_local), jnp.float32),
            pltpu.VMEM((10 * HALF, 128), jnp.float32),
            pltpu.VMEM((8, 128), jnp.float32),
            pltpu.VMEM((n_pts, 8, 128), jnp.float32),
            pltpu.VMEM((8, 128), jnp.float32),
            pltpu.VMEM((n_freq, 8, 128), jnp.float32),
            pltpu.VMEM((128, 128), jnp.float32),
            pltpu.VMEM((rows, 128), jnp.float32),
            dma((n_var,)),
            dma((n_pts,)),
            dma((n_pts,)),
            dma((n_freq,)),
            dma((n_freq,)),
            dma((n_freq,)),
            dma((n_freq,)),
        ],
        compiler_params=pltpu.CompilerParams(collective_id=0, has_side_effects=True),
    )(jnp.transpose(snapshots, (1, 0, 2)), weights.reshape(1, -1), starts, bins.reshape(1, -1))
    modes = rec.reshape(n_freq, per_dev, n_var, tiles, 2, 128)
    modes = jnp.transpose(modes, (1, 4, 2, 0, 3, 5)).reshape(
        per_dev, 2, n_var, n_freq * n_local
    )
    return modes, energy[0, :per_dev]


def solution(mesh):
    n_freq, n_pts = mesh.shape["freq"], mesh.shape["pts"]
    return jax.shard_map(
        functools.partial(body, n_freq, n_pts),
        mesh=mesh,
        in_specs=(P(None, None, ("pts", "freq")), P(("pts", "freq")), P(), P()),
        out_specs=(P("freq", None, None, "pts"), P("freq")),
        check_vma=False,
    )
```

time: 115 us -> 44.8 us (0.39)
  Pallas kernels: 0 us -> 40.5 us
  matrix products: 29.4 us -> 0 us
  waiting for transfers between devices: 26.1 us -> 0 us
  starting transfers between devices: 15.5 us -> 0 us
  local copies, waits for them, and re-layouts: 16.1 us -> 3.53 us
  other arithmetic: 10.2 us -> 0 us
  blocking collectives: 9.74 us -> 0 us
  between operations: 7.66 us -> 0.65 us
    pallas_call x0 -> x1, Pallas kernels: none -> 40.5 us  [body(): pl.pallas_call(functools.partial(kernel, sizes), out_shape=(jax.ShapeDtyp...]
    dot_general x7 -> x0, matrix products: 29.4 us -> none  [the longest x1 10.7 us: gram_of(): jnp.einsum('kacvp,kbcvp->kab', weighted, spec, precision=lax.Precision.HI...]
    all_to_all x2 -> x0, waiting for transfers between devices: 26.1 us -> none  [the longest x1 18.8 us: body(): lax.all_to_all(local_modes, FREQ, split_axis=0, concat_axis=3, tiled=True)]
    all_to_all x2 -> x0, starting transfers between devices: 15.5 us -> none  [the longest x1 11.2 us: from_everyone(): lax.all_to_all(jnp.broadcast_to(value[None], (length, *value.shape)), axi...]
    all_to_all x1 -> x0, blocking collectives: 9.74 us -> none  [from_everyone(): lax.all_to_all(jnp.broadcast_to(value[None], (length, *value.shape)), axi...]
    reduce_sum x22 -> x0, other arithmetic: 5.05 us -> none  [the longest x8 2.81 us: apply_gram(): jnp.sum(gram_re * xr[:, None, :], 2) - jnp.sum(gram_im * xi[:, None, :], 2)]
    mul x3 -> x0, other arithmetic: 3.91 us -> none  [the longest x1 3.58 us: gram_of(): weighted = spec * wts]
    dynamic_slice x5 -> x0, local copies, waits for them, and re-layouts: 3.54 us -> none  [the longest x4 2.96 us: body(): lax.dynamic_slice_in_dim(flat, starts[block], NFFT, 0)]
  transfers between devices with their start and end apart: 2 -> 0, of which waited for: 2 -> 0; matrix products, arithmetic and copies ran while one was open for 3% -> 0% of each run, Pallas kernels for 0% -> 0%
where the time goes in v1:
time: 44.8 us; the launch traced here: 44.7 us
  Pallas kernels  40.5 us (90%)
  local copies, waits for them, and re-layouts  3.53 us (8%)
  between operations  0.65 us (1%)
    pallas_call x1, Pallas kernels, body(): pl.pallas_call(functools.partial(kernel, sizes), out_shape=(jax.ShapeDtyp...  40.5 us
    reshape x1, local copies, waits for them, and re-layouts, body(): jnp.transpose(modes, (1, 4, 2, 0, 3, 5))  1.59 us
    transpose x1, local copies, waits for them, and re-layouts, body(): jnp.transpose(modes, (1, 4, 2, 0, 3, 5))  1.43 us

profile of v1, /device:TPU:32, one launch (start us, length us, event | category | flops | bytes accessed | tf_op | source)
XLA Modules:
  0.0 44.7 jit_solution(10683230155383596639)
XLA Ops:
  0.6 40.5 %shard_map.59 = (f32[1280,128]{1,0:T(8,128)}, f32[1,128]{1,0:T(1,128)}) custom-call(f32[5,256,256]{2,1,0:T(8,128)} %bitcast.10, f32[1,256]{1,0:T(1,128)} %bitcast.12, s32[3]{0:T(128)} %starts.1, s32[1,64]{1,0:T(1,128)} %bitcast.13), custom_call_target="tpu_custom_call" | custom-call | tf_op jit(solution)/shard_map/pallas_call | solution.py:298
  41.1 0.0 copy-start
  41.1 1.4 %copy.6 = f32[2,2,5,32,2,128]{5,4,3,1,2,0:T(2,128)S(1)} copy(f32[2,2,5,32,2,128]{5,1,4,2,0,3:T(2,128)} %bitcast.11) | data formatting | bytes 1310720 | tf_op jit(solution)/shard_map/transpose | solution.py:334
  42.6 1.6 %reshape.19 = f32[2,2,5,8192]{3,1,2,0:T(2,128)} reshape(f32[2,2,5,32,2,128]{5,4,3,1,2,0:T(2,128)S(1)} %copy.6) | data formatting | bytes 1310720 | tf_op jit(solution)/shard_map/reshape | solution.py:334
  44.2 0.0 copy-done
  44.2 0.5 %slice_bitcast_fusion = f32[2]{0:T(128)} fusion(f32[1,128]{1,0:T(1,128)S(1)} %copy-done), kind=kLoop, calls=%fused_computation | loop fusion | bytes 16 | tf_op jit(solution)/shard_map/squeeze | solution.py:337
Async XLA Ops:
  41.1 3.0 %copy-start = (f32[1,128]{1,0:T(1,128)S(1)}, f32[1,128]{1,0:T(1,128)}, u32[]{:S(2)}) copy-start(f32[1,128]{1,0:T(1,128)} %get-tuple-element.5) | copy-start | bytes 1540

commit v2 on v1

--- a/solution.py
+++ b/solution.py
@@ -330,10 +330,9 @@
         ],
         compiler_params=pltpu.CompilerParams(collective_id=0, has_side_effects=True),
     )(jnp.transpose(snapshots, (1, 0, 2)), weights.reshape(1, -1), starts, bins.reshape(1, -1))
-    modes = rec.reshape(n_freq, per_dev, n_var, tiles, 2, 128)
-    modes = jnp.transpose(modes, (1, 4, 2, 0, 3, 5)).reshape(
-        per_dev, 2, n_var, n_freq * n_local
-    )
+    modes = rec.reshape(n_freq, per_dev * n_var, 2 * tiles, 128)
+    modes = jnp.transpose(modes, (1, 0, 2, 3)).reshape(per_dev, n_var, n_freq * tiles, 2, 128)
+    modes = jnp.transpose(modes, (0, 3, 1, 2, 4)).reshape(per_dev, 2, n_var, n_freq * n_local)
     return modes, energy[0, :per_dev]
 
 

time: 44.8 us -> 43.9 us (0.980)
  local copies, waits for them, and re-layouts: 3.53 us -> 2.58 us
    transpose x1 -> x0, local copies, waits for them, and re-layouts: 1.43 us -> none  [body(): jnp.transpose(modes, (1, 4, 2, 0, 3, 5))]
    reshape x1, local copies, waits for them, and re-layouts: 1.59 us -> 2.06 us  [body(): modes = rec.reshape(n_freq, per_dev * n_var, 2 * tiles, 128)]
where the time goes in v2:
time: 43.9 us; the launch traced here: 43.7 us
  Pallas kernels  40.5 us (92%)
  local copies, waits for them, and re-layouts  2.58 us (6%)
  between operations  0.65 us (1%)
    pallas_call x1, Pallas kernels, body(): pl.pallas_call(functools.partial(kernel, sizes), out_shape=(jax.ShapeDtyp...  40.5 us
    reshape x1, local copies, waits for them, and re-layouts, body(): modes = rec.reshape(n_freq, per_dev * n_var, 2 * tiles, 128)  2.06 us

profile of v2, /device:TPU:32, one launch (start us, length us, event | category | flops | bytes accessed | tf_op | source)
XLA Modules:
  0.0 43.7 jit_solution(12878022917909848179)
XLA Ops:
  0.6 40.5 %shard_map.59 = (f32[1280,128]{1,0:T(8,128)}, f32[1,128]{1,0:T(1,128)}) custom-call(f32[5,256,256]{2,1,0:T(8,128)} %bitcast.13, f32[1,256]{1,0:T(1,128)} %bitcast.16, s32[3]{0:T(128)} %starts.1, s32[1,64]{1,0:T(1,128)} %bitcast.17), custom_call_target="tpu_custom_call" | custom-call | tf_op jit(solution)/shard_map/pallas_call | solution.py:298
  41.1 0.0 copy-start
  41.1 2.1 %copy.6 = f32[32,10,4,128]{3,2,0,1:T(4,128)} copy(f32[32,10,4,128]{3,2,1,0:T(4,128)} %bitcast.15) | data formatting | bytes 1310720 | tf_op jit(solution)/shard_map/reshape | solution.py:333
  43.2 0.0 copy-done
  43.2 0.5 %slice_bitcast_fusion = f32[2]{0:T(128)} fusion(f32[1,128]{1,0:T(1,128)S(1)} %copy-done), kind=kLoop, calls=%fused_computation | loop fusion | bytes 16 | tf_op jit(solution)/shard_map/squeeze | solution.py:336
Async XLA Ops:
  41.1 2.1 %copy-start = (f32[1,128]{1,0:T(1,128)S(1)}, f32[1,128]{1,0:T(1,128)}, u32[]{:S(2)}) copy-start(f32[1,128]{1,0:T(1,128)} %get-tuple-element.5) | copy-start | bytes 1540

commit v3 on v1

--- a/solution.py
+++ b/solution.py
@@ -63,40 +63,47 @@
     ]
 
 
-def exchange(value, mine, axis, length, source, landed, sends, recvs):
-    me = lax.axis_index(axis)
+def exchange(value, slot, group, source, landed, sent, came):
     source[...] = value
-    landed[me] = value
-
-    def copy(peer, slot):
-        return pltpu.make_async_remote_copy(
+    landed[slot] = value
+    for peer in group:
+        pltpu.make_async_remote_copy(
             src_ref=source,
             dst_ref=landed.at[slot],
-            send_sem=sends.at[peer],
-            recv_sem=recvs.at[slot],
-            device_id={axis: peer},
+            send_sem=sent,
+            recv_sem=came,
+            device_id=peer,
             device_id_type=MESH,
-        )
-
-    def send(d, carry):
-        copy(lax.rem(me + length - d, length), me).start()
-        return carry
-
-    def wait(d, carry):
-        peer = lax.rem(me + d, length)
-        copy(peer, peer).wait_recv()
-        return carry
-
-    def drain(d, carry):
-        copy(lax.rem(me + length - d, length), me).wait_send()
-        return carry
-
-    lax.fori_loop(1, length, send, 0)
-    lax.fori_loop(1, length, wait, 0)
+        ).start()
+    held = landed.at[pl.ds(0, len(group))]
+    pltpu.make_async_copy(held, held, came).wait()
     total = landed[0]
-    for peer in range(1, length):
-        total += landed[peer]
-    return total, lambda: lax.fori_loop(1, length, drain, 0)
+    for n in range(1, len(group) + 1):
+        total += landed[n]
+    return total, lambda: pltpu.make_async_copy(held, held, sent).wait()
+
+
+def groups_of(sizes):
+    nx, nz, ny = sizes
+    f, p = lax.axis_index("freq"), lax.axis_index("pts")
+    x, z, y, core = f // nz, lax.rem(f, nz), p // 2, lax.rem(p, 2)
+
+    def far(d, n):
+        return min(d, n - d)
+
+    steps = [(i, j) for i in range(nx) for j in range(ny) if i or j]
+    steps.sort(key=lambda s: -far(s[0], nx) - far(s[1], ny))
+    plane = [
+        {"freq": lax.rem(x + i, nx) * nz + z, "pts": lax.rem(y + j, ny) * 2 + core}
+        for i, j in steps
+    ]
+    steps = [(i, j) for i in range(nz) for j in range(2) if i or j]
+    steps.sort(key=lambda s: -far(s[0], nz) - 0.5 * s[1])
+    line = [
+        {"freq": x * nz + lax.rem(z + i, nz), "pts": y * 2 + lax.rem(core + j, 2)}
+        for i, j in steps
+    ]
+    return (x * ny + y, plane), (z * 2 + core, line)
 
 
 def leading(total):
@@ -135,39 +142,38 @@
 
 
 def kernel(
-    sizes, snap, wts, starts, bins, rec, energy_out,
-    xbuf, lhs, rhs, spec, acc, g1, g1r, g2, g2r, coef, send,
-    load_sem, s1, r1, s2, r2, s3, r3,
+    sizes, split_sizes, snap, wts_in, starts_in, bins_in, rec, energy_out,
+    wts, starts, bins, xbuf, lhs, rhs, spec, acc, g1, g1r, g2, g2r, coef, send,
+    load_sem, small_sem, s1, r1, s2, r2, s3, r3,
 ):
     n_freq, n_pts, kf, n_var, n_time, n_local = sizes
     per_dev = kf // n_freq
-    me_f, me_p = lax.axis_index("freq"), lax.axis_index("pts")
+    me_f = lax.axis_index("freq")
 
     def load(v):
         return pltpu.make_async_copy(snap.at[v], xbuf.at[v], load_sem.at[v])
 
+    small = [
+        pltpu.make_async_copy(source, target, small_sem.at[n])
+        for n, (source, target) in enumerate(
+            ((bins_in, bins), (starts_in, starts), (wts_in, wts))
+        )
+    ]
+    for copy in small:
+        copy.start()
     for v in range(n_var):
         load(v).start()
 
     barrier = pltpu.get_barrier_semaphore()
-
-    def greet(axis, me, length):
-        def one(d, carry):
-            pl.semaphore_signal(
-                barrier,
-                inc=1,
-                device_id={axis: lax.rem(me + d, length)},
-                device_id_type=MESH,
-            )
-            return carry
-
-        lax.fori_loop(1, length, one, 0)
-
-    greet("freq", me_f, n_freq)
-    greet("pts", me_p, n_pts)
-
+    near_group, far_group = groups_of(split_sizes)
+    everyone = far_group[1] + near_group[1]
+    for peer in everyone:
+        pl.semaphore_signal(barrier, inc=1, device_id=peer, device_id_type=MESH)
+
+    acc[...] = jnp.zeros_like(acc)
+    for copy in small:
+        copy.wait()
     fill_tables(starts, bins, lhs, kf, n_time)
-    acc[...] = jnp.zeros_like(acc)
 
     def transform(v, carry):
         load(v).wait()
@@ -215,9 +221,9 @@
     for n in range(5):
         mine = jnp.where(sublane == n, by_lane[:, n * 128 : n * 128 + 128], mine)
 
-    pl.semaphore_wait(barrier, n_freq + n_pts - 2)
-    near, drain_near = exchange(mine, me_p, "pts", n_pts, g1, g1r, s1, r1)
-    total, drain_far = exchange(near, me_f, "freq", n_freq, g2, g2r, s2, r2)
+    pl.semaphore_wait(barrier, len(everyone))
+    near, drain_near = exchange(mine[:5], *near_group, g1, g1r, s1, r1)
+    total, drain_far = exchange(near, *far_group, g2, g2r, s2, r2)
     total = total / float(n_freq * n_pts * n_local * n_var)
 
     coefs, energy = leading(total)
@@ -236,8 +242,8 @@
         return pltpu.make_async_remote_copy(
             src_ref=send.at[pl.ds(dest * rows, rows), :],
             dst_ref=rec.at[pl.ds(slot * rows, rows), :],
-            send_sem=s3.at[dest],
-            recv_sem=r3.at[slot],
+            send_sem=s3,
+            recv_sem=r3,
             device_id={"freq": dest},
             device_id_type=MESH,
         )
@@ -271,76 +277,91 @@
 
     lax.fori_loop(0, n_oct, modes, 0)
 
-    def take(d, carry):
-        peer = lax.rem(me_f + d, n_freq)
-        give(peer, peer).wait_recv()
-        return carry
-
-    def sent(d, carry):
-        give(lax.rem(me_f + d, n_freq), me_f).wait_send()
-        return carry
-
-    lax.fori_loop(1, n_freq, take, 0)
-    lax.fori_loop(1, n_freq, sent, 0)
+    others = rec.at[pl.ds(0, (n_freq - 1) * rows), :]
+    pltpu.make_async_copy(others, others, r3).wait()
+    pltpu.make_async_copy(others, others, s3).wait()
     drain_near()
     drain_far()
 
 
-def body(n_freq, n_pts, snapshots, weights, starts, bins):
+def write_out(groups, n_freq, lines, per_dev, rec, row, modes, energy, sems):
+    copies = [
+        pltpu.make_async_copy(rec.at[:, g], modes.at[g], sems.at[g]) for g in range(groups)
+    ]
+    for copy in copies:
+        copy.start()
+    energy[...] = row[0, :per_dev]
+    for copy in copies:
+        copy.wait()
+
+
+def body(n_freq, n_pts, nz, snapshots, weights, starts, bins):
     n_time, n_var, n_local = snapshots.shape
     kf = bins.shape[0]
     per_dev = kf // n_freq
     tiles = n_local // 128
     rows = kf * n_var * 2 * tiles
     sizes = (n_freq, n_pts, kf, n_var, n_time, n_local)
-    vmem = pl.BlockSpec(memory_space=pltpu.VMEM)
+    split_sizes = (n_freq // nz, nz, n_pts // 2)
+    near, far = split_sizes[0] * split_sizes[2], 2 * nz
+    vmem, anywhere = (pl.BlockSpec(memory_space=m) for m in (pltpu.VMEM, pl.ANY))
     dma = pltpu.SemaphoreType.DMA
     rec, energy = pl.pallas_call(
-        functools.partial(kernel, sizes),
+        functools.partial(kernel, sizes, split_sizes),
         out_shape=(
-            jax.ShapeDtypeStruct((rows, 128), jnp.float32),
-            jax.ShapeDtypeStruct((1, 128), jnp.float32),
+            pltpu.VMEM((rows, 128), jnp.float32),
+            pltpu.VMEM((1, 128), jnp.float32),
         ),
-        in_specs=[
-            pl.BlockSpec(memory_space=pl.ANY),
-            vmem,
-            pl.BlockSpec(memory_space=pltpu.SMEM),
-            vmem,
-        ],
+        in_specs=[anywhere] * 4,
         out_specs=(vmem, vmem),
         scratch_shapes=[
+            pltpu.VMEM((1, n_local), jnp.float32),
+            pltpu.SMEM((NB,), jnp.int32),
+            pltpu.VMEM((1, kf), jnp.int32),
             pltpu.VMEM((n_var, n_time, n_local), jnp.float32),
             pltpu.VMEM((2 * NB * kf, 3 * n_time), jnp.bfloat16),
             pltpu.VMEM((3 * n_time, n_local), jnp.bfloat16),
             pltpu.VMEM((n_var, 2 * NB * kf, n_local), jnp.float32),
             pltpu.VMEM((10 * HALF, 128), jnp.float32),
-            pltpu.VMEM((8, 128), jnp.float32),
-            pltpu.VMEM((n_pts, 8, 128), jnp.float32),
-            pltpu.VMEM((8, 128), jnp.float32),
-            pltpu.VMEM((n_freq, 8, 128), jnp.float32),
+            pltpu.VMEM((5, 128), jnp.float32),
+            pltpu.VMEM((near, 5, 128), jnp.float32),
+            pltpu.VMEM((5, 128), jnp.float32),
+            pltpu.VMEM((far, 5, 128), jnp.float32),
             pltpu.VMEM((128, 128), jnp.float32),
             pltpu.VMEM((rows, 128), jnp.float32),
             dma((n_var,)),
-            dma((n_pts,)),
-            dma((n_pts,)),
-            dma((n_freq,)),
-            dma((n_freq,)),
-            dma((n_freq,)),
-            dma((n_freq,)),
-        ],
+            dma((3,)),
+        ]
+        + [pltpu.SemaphoreType.DMA(())] * 6,
         compiler_params=pltpu.CompilerParams(collective_id=0, has_side_effects=True),
     )(jnp.transpose(snapshots, (1, 0, 2)), weights.reshape(1, -1), starts, bins.reshape(1, -1))
-    modes = rec.reshape(n_freq, per_dev, n_var, tiles, 2, 128)
-    modes = jnp.transpose(modes, (1, 4, 2, 0, 3, 5)).reshape(
+    groups = per_dev * n_var
+    modes, energy = pl.pallas_call(
+        functools.partial(write_out, groups, n_freq, 2 * tiles, per_dev),
+        out_shape=(
+            jax.ShapeDtypeStruct((groups, n_freq, 2 * tiles, 128), jnp.float32),
+            jax.ShapeDtypeStruct((per_dev,), jnp.float32),
+        ),
+        in_specs=[vmem, vmem],
+        out_specs=(pl.BlockSpec(memory_space=pl.ANY), vmem),
+        scratch_shapes=[dma((groups,))],
+    )(
+        pltpu.with_memory_space_constraint(
+            rec.reshape(n_freq, groups, 2 * tiles, 128), pltpu.VMEM
+        ),
+        pltpu.with_memory_space_constraint(energy, pltpu.VMEM),
+    )
+    modes = modes.reshape(per_dev, n_var, n_freq * tiles, 2, 128)
+    modes = jnp.transpose(modes, (0, 3, 1, 2, 4)).reshape(
         per_dev, 2, n_var, n_freq * n_local
     )
-    return modes, energy[0, :per_dev]
+    return modes, energy
 
 
 def solution(mesh):
     n_freq, n_pts = mesh.shape["freq"], mesh.shape["pts"]
     return jax.shard_map(
-        functools.partial(body, n_freq, n_pts),
+        functools.partial(body, n_freq, n_pts, 8 if n_freq % 8 == 0 else 2),
         mesh=mesh,
         in_specs=(P(None, None, ("pts", "freq")), P(("pts", "freq")), P(), P()),
         out_specs=(P("freq", None, None, "pts"), P("freq")),

time: 44.8 us -> 38.5 us (0.86)
  local copies, waits for them, and re-layouts: 3.53 us -> 0 us
  Pallas kernels: 40.5 us -> 37.3 us
    pallas_call x1 -> x2, Pallas kernels: 40.5 us -> 37.3 us  [the longest x1 35.9 us: body(): pl.pallas_call(functools.partial(kernel, sizes, split_sizes), out_shape=(...]
    reshape x1 -> x0, local copies, waits for them, and re-layouts: 1.59 us -> none  [body(): jnp.transpose(modes, (1, 4, 2, 0, 3, 5))]
    transpose x1 -> x0, local copies, waits for them, and re-layouts: 1.43 us -> none  [body(): jnp.transpose(modes, (1, 4, 2, 0, 3, 5))]
    squeeze x1 -> x0, local copies, waits for them, and re-layouts: 0.51 us -> none  [body(): return (modes, energy[0, :per_dev])]
where the time goes in v3:
time: 38.5 us; the launch traced here: 38 us
  Pallas kernels  37.3 us (97%)
  between operations  0.64 us (2%)
    pallas_call x1, Pallas kernels, body(): pl.pallas_call(functools.partial(kernel, sizes, split_sizes), out_shape=(...  35.9 us
    pallas_call x1, Pallas kernels, body(): pl.pallas_call(functools.partial(write_out, groups, n_freq, 2 * tiles, pe...  1.42 us

profile of v3, /device:TPU:32, one launch (start us, length us, event | category | flops | bytes accessed | tf_op | source)
XLA Modules:
  0.0 38.0 jit_solution(12045732227170072527)
XLA Ops:
  0.6 35.9 %shard_map.59 = (f32[1280,128]{1,0:T(8,128)S(1)}, f32[1,128]{1,0:T(1,128)S(1)}) custom-call(f32[5,256,256]{2,1,0:T(8,128)} %bitcast.10, f32[1,256]{1,0:T(1,128)} %bitcast.11, s32[3]{0:T(128)} %starts_in.1, s32[1,64]{1,0:T(1,128)} %bitcast.12), custom_call_target="tpu_custom_call" | custom-call | tf_op jit(solution)/shard_map/pallas_call | solution.py:309
  36.6 1.4 %shard_map.60 = (f32[10,32,4,128]{3,2,1,0:T(4,128)}, f32[2]{0:T(128)}) custom-call(f32[32,10,4,128]{3,2,1,0:T(4,128)S(1)} %bitcast.9, f32[1,128]{1,0:T(1,128)S(1)} %get-tuple-element.7.row), custom_call_target="tpu_custom_call" | custom-call | tf_op jit(solution)/shard_map/pallas_call | solution.py:339

commit v4 on v3

v4 whole, which is shorter than its diff:
```python
import functools
import math

import jax
import jax.numpy as jnp
from jax import lax
from jax.experimental import pallas as pl
from jax.experimental.pallas import tpu as pltpu
from jax.sharding import PartitionSpec as P

NFFT = 128
NB = 3
ITERS = 8
LENGTH_Z = 8
HALF = 64
PAIRS = ((0, 1), (0, 2), (1, 2))
MESH = pl.DeviceIdType.MESH


def half_angle(steps):
    h = steps.astype(jnp.float32) * (math.pi / NFFT)
    z = h * h
    s = jnp.float32(1.0 / math.factorial(13))
    for n in (11, 9, 7, 5, 3, 1):
        s = (1.0 if (n // 2) % 2 == 0 else -1.0) / math.factorial(n) + s * z
    c = jnp.float32(1.0 / math.factorial(12))
    for n in (10, 8, 6, 4, 2, 0):
        c = (1.0 if (n // 2) % 2 == 0 else -1.0) / math.factorial(n) + c * z
    return s * h, c


def split(value):
    high = value.astype(jnp.bfloat16)
    return high, (value - high.astype(jnp.float32)).astype(jnp.bfloat16)


def fill_tables(starts, bins, lhs, kf, n_time, per_dev):
    n_dev = kf // per_dev
    slot = lax.broadcasted_iota(jnp.int32, (kf, kf), 0)
    slot = lax.rem(slot, n_dev) * per_dev + slot // n_dev
    here = lax.broadcasted_iota(jnp.int32, (kf, kf), 1) == slot
    row = jnp.broadcast_to(bins[...].astype(jnp.float32), (kf, kf))
    column = jnp.sum(jnp.where(here, row, 0.0), axis=1, keepdims=True).astype(jnp.int32)
    lane = lax.broadcasted_iota(jnp.int32, (kf, NFFT), 1)
    time = lax.broadcasted_iota(jnp.int32, (1, n_time), 1)
    scale = 1.0 / math.sqrt(NFFT * 3 / 8)
    for block in range(NB):
        t = time - starts[block]
        sin_w, _ = half_angle(jnp.clip(64 - jnp.abs(t - 64), 0, 64))
        window = sin_w * sin_w * scale
        window = jnp.where((t >= 0) & (t < NFFT), window, 0.0)
        t = lane - starts[block]
        sin_h, cos_h = half_angle((((column * t) + 64) & (NFFT - 1)) - 64)
        for part, table in enumerate((1.0 - 2.0 * sin_h * sin_h, -2.0 * sin_h * cos_h)):
            rows = pl.ds((2 * block + part) * kf, kf)
            for n in range(n_time // NFFT):
                high, low = split(table * window[:, n * NFFT : (n + 1) * NFFT])
                for third, value in enumerate((high, high, low)):
                    at = third * n_time + n * NFFT
                    lhs[rows, at : at + NFFT] = value


def eight_bins(spec, kf, octet, v, cut):
    return [
        [spec[v, pl.ds((2 * b + part) * kf + octet * 8, 8), cut] for part in range(2)]
        for b in range(NB)
    ]


def exchange(slot, group, source, landed, sent, came):
    shared = sum(number == 0 for _, number in group)

    def wait(count, sem):
        held = landed.at[pl.ds(0, count)]
        pltpu.make_async_copy(held, held, sem).wait()

    def start(value):
        source[...] = value
        landed[slot] = value
        for peer, number in group:
            pltpu.make_async_remote_copy(
                src_ref=source,
                dst_ref=landed.at[slot],
                send_sem=sent,
                recv_sem=came.at[number],
                device_id=peer,
                device_id_type=MESH,
            ).start()

    def one(number):
        wait(1, came.at[number])

    def finish():
        wait(shared, came.at[0])
        total = landed[0]
        for n in range(1, len(group) + 1):
            total += landed[n]
        return total

    def drain():
        wait(len(group), sent)

    return start, one, finish, drain


def groups_of(sizes):
    nx, nz, ny = sizes
    f, p = lax.axis_index("freq"), lax.axis_index("pts")
    x, z, y, core = f // nz, lax.rem(f, nz), p // 2, lax.rem(p, 2)

    def far(d, n):
        return min(d, n - d)

    steps = [(i, j) for i in range(nx) for j in range(ny) if i or j]
    steps.sort(key=lambda s: -far(s[0], nx) - far(s[1], ny))
    plane = [
        ({"freq": lax.rem(x + i, nx) * nz + z, "pts": lax.rem(y + j, ny) * 2 + core}, 0 if j else i)
        for i, j in steps
    ]
    steps = [(i, j) for i in range(nz) for j in range(2) if i or j]
    steps.sort(key=lambda s: -far(s[0], nz) - 0.5 * s[1])
    line = [
        ({"freq": x * nz + lax.rem(z + i, nz), "pts": y * 2 + lax.rem(core + j, 2)}, 0)
        for i, j in steps
    ]
    return (x * ny + y, plane), (z * 2 + core, line)


def leading(total):
    other = pltpu.roll(total, HALF, 1)
    q = [(total if n % 2 == 0 else other)[n // 2 : n // 2 + 1, :] for n in range(9)]
    re = {(a, a): q[a] for a in range(NB)}
    im = {}
    for n, (a, c) in enumerate(PAIRS):
        re[a, c] = re[c, a] = q[3 + n]
        im[a, c], im[c, a] = q[6 + n], -q[6 + n]

    def apply(xr, xi):
        ur, ui = [], []
        for a in range(NB):
            r, i = re[a, a] * xr[a], re[a, a] * xi[a]
            for c in range(NB):
                if c != a:
                    r = r + (re[a, c] * xr[c] - im[a, c] * xi[c])
                    i = i + (re[a, c] * xi[c] + im[a, c] * xr[c])
            ur.append(r)
            ui.append(i)
        return ur, ui

    def step(_, x):
        ur, ui = apply(x[:NB], x[NB:])
        norm = sum(r * r + i * i for r, i in zip(ur, ui))
        scale = lax.rsqrt(norm)
        return tuple(r * scale for r in ur) + tuple(i * scale for i in ui)

    one = jnp.ones_like(q[0])
    x = lax.fori_loop(0, ITERS, step, (one,) * NB + (one - one,) * NB)
    ur, ui = apply(x[:NB], x[NB:])
    energy = sum(x[a] * ur[a] + x[NB + a] * ui[a] for a in range(NB))
    factor = 1.0 / jnp.sqrt(jnp.maximum(energy, 0.25))
    return [v * factor for v in x], energy


def kernel(
    sizes, split_sizes, early, snap, wts_in, starts_in, bins_in, rec, tail, energy_out,
    wts, starts, bins, xbuf, lhs, rhs, spec, acc, g1, g1r, g2, g2r, coef, send, ahead, ahead_r,
    load_sem, small_sem, s1, r1, s2, r2, s3, r3, s4, r4,
):
    n_freq, n_pts, kf, n_var, n_time, n_local = sizes
    nx, nz, _ = split_sizes
    per_dev = kf // n_freq
    me_f = lax.axis_index("freq")
    n_oct, wide = n_freq // 8, 8
    cuts = [slice(128 * n, 128 * n + 128) for n in range(n_local // 128)]
    units = [(v, cut) for v in range(n_var) for cut in cuts]
    late, soon = units[: len(units) - early], units[len(units) - early :]

    def load(v):
        return pltpu.make_async_copy(snap.at[v], xbuf.at[v], load_sem.at[v])

    small = [
        pltpu.make_async_copy(source, target, small_sem.at[n])
        for n, (source, target) in enumerate(
            ((bins_in, bins), (starts_in, starts), (wts_in, wts))
        )
    ]
    for copy in small:
        copy.start()
    for v in range(n_var):
        load(v).start()

    barrier = pltpu.get_barrier_semaphore()
    near_group, far_group = groups_of(split_sizes)
    everyone = far_group[1] + near_group[1]
    for peer, _ in everyone:
        pl.semaphore_signal(barrier, inc=1, device_id=peer, device_id_type=MESH)

    acc[...] = jnp.zeros_like(acc)
    for copy in small:
        copy.wait()
    fill_tables(starts, bins, lhs, kf, n_time, per_dev)

    def centre(v, slot):
        x = xbuf[v]
        x = x - jnp.sum(x, axis=0, keepdims=True) * (1.0 / n_time)
        high, low = split(x)
        rhs[slot, 0:n_time, :] = high
        rhs[slot, n_time : 2 * n_time, :] = low
        rhs[slot, 2 * n_time : 3 * n_time, :] = high

    def gram(v):
        ws = [jnp.broadcast_to(wts[:, cut], (8, 128)) for cut in cuts]
        for octet in range(kf // 8):
            sums = [acc[pl.ds(n * HALF + octet * 8, 8), :] for n in range(9)]
            for w, cut in zip(ws, cuts):
                s = eight_bins(spec, kf, octet, v, cut)
                wt = [[w * part for part in one] for one in s]
                terms = [wt[a][0] * s[a][0] + wt[a][1] * s[a][1] for a in range(NB)]
                terms += [wt[a][0] * s[c][0] + wt[a][1] * s[c][1] for a, c in PAIRS]
                terms += [wt[a][0] * s[c][1] - wt[a][1] * s[c][0] for a, c in PAIRS]
                sums = [x + y for x, y in zip(sums, terms)]
            for n in range(9):
                acc[pl.ds(n * HALF + octet * 8, 8), :] = sums[n]

    def transform(v):
        spec[v] = jnp.dot(lhs[...], rhs[v], preferred_element_type=jnp.float32)

    for v in range(n_var):
        load(v).wait()
    centre(0, 0)
    for v in range(n_var):
        transform(v)
        if v + 1 < n_var:
            centre(v + 1, v + 1)
        if v:
            gram(v - 1)
    gram(n_var - 1)

    parts = acc[...]
    first = parts.astype(jnp.bfloat16)
    second, third = split(parts - first.astype(jnp.float32))
    by_lane = lax.dot_general(
        jnp.ones((8, 3 * 128), jnp.bfloat16),
        jnp.concatenate([first, second, third], axis=1),
        (((1,), (1,)), ((), ())),
        preferred_element_type=jnp.float32,
    )
    sublane = lax.broadcasted_iota(jnp.int32, (8, 128), 0)
    mine = jnp.zeros((8, 128), jnp.float32)
    for n in range(5):
        mine = jnp.where(sublane == n, by_lane[:, n * 128 : n * 128 + 128], mine)

    start_near, one_near, finish_near, drain_near = exchange(*near_group, g1, g1r, s1, r1)
    start_far, _, finish_far, drain_far = exchange(*far_group, g2, g2r, s2, r2)

    pitch = per_dev * early * 2 * NB

    def lead(dest, slot):
        return pltpu.make_async_remote_copy(
            src_ref=ahead.at[pl.ds(dest * pitch, pitch), :],
            dst_ref=ahead_r.at[pl.ds(slot * pitch, pitch), :],
            send_sem=s4,
            recv_sem=r4,
            device_id={"freq": dest},
            device_id_type=MESH,
        )

    def pack(octet, carry):
        for kk in range(per_dev):
            for n, (v, cut) in enumerate(soon):
                s = eight_bins(spec, kf, kk * n_oct + octet, v, cut)
                for b in range(NB):
                    for part in range(2):
                        at = octet * (8 * pitch) + ((kk * early + n) * NB + b) * 2 + part
                        ahead[pl.ds(at, wide, stride=pitch), :] = s[b][part]
        return carry

    if early:
        lax.fori_loop(0, n_oct, pack, 0)
        mine_rows = pl.ds(me_f * pitch, pitch)
        ahead_r[mine_rows, :] = ahead[mine_rows, :]

    x, z = me_f // nz, lax.rem(me_f, nz)

    def send_ahead(dx):
        for dz in range(nz):
            if dx or dz:
                dest = lax.rem(x + dx, nx) * nz + lax.rem(z + dz, nz)
                lead(dest, me_f).start()

    pl.semaphore_wait(barrier, len(everyone))
    start_near(mine[:5])
    send_ahead(0)
    order = sorted(range(1, nx), key=lambda d: min(d, nx - d))
    for n, dx in enumerate(order):
        one_near(nx - dx)
        if n < 1:
            send_ahead(dx)
    near = finish_near()
    start_far(near)
    for dx in order[1:]:
        send_ahead(dx)
    total = finish_far()
    total = total / float(n_freq * n_pts * n_local * n_var)

    coefs, energy = leading(total)
    lane = lax.broadcasted_iota(jnp.int32, (1, 128), 1)
    for kk in range(per_dev):
        turned = pltpu.roll(energy, lax.rem(256 + kk - kk * n_freq - me_f, 128), 1)
        row = turned if kk == 0 else jnp.where(lane == kk, turned, row)
    energy_out[...] = row
    table = jnp.zeros((128, 128), jnp.float32)
    high = lax.broadcasted_iota(jnp.int32, (128, 128), 0)
    for n, c in enumerate(coefs):
        table = jnp.where(high == n, jnp.broadcast_to(c, (128, 128)), table)
    coef[...] = jnp.transpose(table)

    part_rows = len(late) * 2
    rows = per_dev * part_rows
    slot_rows = rows + 8

    def give(dest, slot):
        return pltpu.make_async_remote_copy(
            src_ref=send.at[pl.ds(dest * slot_rows, rows), :],
            dst_ref=rec.at[pl.ds(slot * rows, rows), :],
            send_sem=s3,
            recv_sem=r3,
            device_id={"freq": dest},
            device_id_type=MESH,
        )

    def spread(c):
        return [jnp.broadcast_to(c[:, n : n + 1], (8, 128)) for n in range(2 * NB)]

    def combine(c, s):
        re = sum(c[b] * s[b][0] - c[NB + b] * s[b][1] for b in range(NB))
        im = sum(c[b] * s[b][1] + c[NB + b] * s[b][0] for b in range(NB))
        return re, im

    def modes(i, carry):
        octet = lax.rem(me_f // 8 + 1 + i, n_oct)
        for kk in range(per_dev):
            c = spread(coef[pl.ds(kk * n_freq + octet * 8, 8), :])
            for n, (v, cut) in enumerate(late):
                s = eight_bins(spec, kf, kk * n_oct + octet, v, cut)
                for part, value in enumerate(combine(c, s)):
                    at = octet * (8 * slot_rows) + kk * part_rows + 2 * n + part
                    send[pl.ds(at, wide, stride=slot_rows), :] = value
        for d in range(wide):
            dest = octet * 8 + d

            @pl.when(dest != me_f)
            def _():
                give(dest, me_f).start()

            @pl.when(dest == me_f)
            def _():
                rec[pl.ds(me_f * rows, rows), :] = send[pl.ds(me_f * slot_rows, rows), :]

        return carry

    lax.fori_loop(0, n_oct, modes, 0)

    if early:
        theirs = ahead_r.at[pl.ds(0, (n_freq - 1) * pitch), :]
        pltpu.make_async_copy(theirs, theirs, r4).wait()
        for kk in range(per_dev):
            c = coef[pl.ds(kk * n_freq + me_f, 1), :]
            c = spread(jnp.broadcast_to(c, (8, 128)))
            for octet in range(n_oct):
                for n in range(early):
                    s = [
                        [
                            ahead_r[
                                pl.ds(
                                    octet * 8 * pitch + ((kk * early + n) * NB + b) * 2 + part,
                                    wide,
                                    stride=pitch,
                                ),
                                :,
                            ]
                            for part in range(2)
                        ]
                        for b in range(NB)
                    ]
                    for part, value in enumerate(combine([q for q in c], s)):
                        at = octet * 16 * per_dev * early + (kk * early + n) * 2 + part
                        tail[pl.ds(at, wide, stride=2 * per_dev * early), :] = value

    others = rec.at[pl.ds(0, (n_freq - 1) * rows), :]
    pltpu.make_async_copy(others, others, r3).wait()
    pltpu.make_async_copy(others, others, s3).wait()
    if early:
        pltpu.make_async_copy(theirs, theirs, s4).wait()
    drain_near()
    drain_far()


def write_out(sizes, early, rec, tail, row, modes, energy, sems):
    per_dev, n_var, tiles = sizes
    left = n_var * tiles - early
    copies = []

    def add(source, target):
        copies.append(pltpu.make_async_copy(source, target, sems.at[len(copies)]))

    for kk in range(per_dev):
        for v in range(n_var):
            held = modes.at[kk * n_var + v]
            if (v + 1) * tiles <= left:
                add(rec.at[:, kk, pl.ds(v * tiles, tiles)], held)
            elif v * tiles >= left:
                add(tail.at[:, pl.ds(kk * early + v * tiles - left, tiles)], held)
            else:
                cut = left - v * tiles
                add(rec.at[:, kk, pl.ds(v * tiles, cut)], held.at[:, pl.ds(0, cut)])
                add(
                    tail.at[:, pl.ds(kk * early, tiles - cut)],
                    held.at[:, pl.ds(cut, tiles - cut)],
                )
    for copy in copies:
        copy.start()
    energy[...] = row[0, :per_dev]
    for copy in copies:
        copy.wait()


def body(n_freq, n_pts, nz, snapshots, weights, starts, bins):
    n_time, n_var, n_local = snapshots.shape
    kf = bins.shape[0]
    per_dev = kf // n_freq
    tiles = n_local // 128
    early = 2
    rows = kf * (n_var * tiles - early) * 2
    ahead = max(kf * early * 2 * NB, 8)
    tail_rows = max(kf * early * 2, n_freq * 2)
    sizes = (n_freq, n_pts, kf, n_var, n_time, n_local)
    split_sizes = (n_freq // nz, nz, n_pts // 2)
    near, far = split_sizes[0] * split_sizes[2], 2 * nz
    vmem, anywhere = (pl.BlockSpec(memory_space=m) for m in (pltpu.VMEM, pl.ANY))
    dma = pltpu.SemaphoreType.DMA
    rec, tail, energy = pl.pallas_call(
        functools.partial(kernel, sizes, split_sizes, early),
        out_shape=(
            pltpu.VMEM((rows, 128), jnp.float32),
            pltpu.VMEM((tail_rows, 128), jnp.float32),
            pltpu.VMEM((1, 128), jnp.float32),
        ),
        in_specs=[anywhere] * 4,
        out_specs=(vmem, vmem, vmem),
        scratch_shapes=[
            pltpu.VMEM((1, n_local), jnp.float32),
            pltpu.SMEM((NB,), jnp.int32),
            pltpu.VMEM((1, kf), jnp.int32),
            pltpu.VMEM((n_var, n_time, n_local), jnp.float32),
            pltpu.VMEM((2 * NB * kf, 3 * n_time), jnp.bfloat16),
            pltpu.VMEM((n_var, 3 * n_time, n_local), jnp.bfloat16),
            pltpu.VMEM((n_var, 2 * NB * kf, n_local), jnp.float32),
            pltpu.VMEM((10 * HALF, 128), jnp.float32),
            pltpu.VMEM((5, 128), jnp.float32),
            pltpu.VMEM((near, 5, 128), jnp.float32),
            pltpu.VMEM((5, 128), jnp.float32),
            pltpu.VMEM((far, 5, 128), jnp.float32),
            pltpu.VMEM((128, 128), jnp.float32),
            pltpu.VMEM((rows + 8 * n_freq, 128), jnp.float32),
            pltpu.VMEM((ahead, 128), jnp.float32),
            pltpu.VMEM((ahead, 128), jnp.float32),
            dma((n_var,)),
            dma((3,)),
        ]
        + [dma(()), dma((split_sizes[0],)), dma(()), dma((1,))]
        + [dma(())] * 4,
        compiler_params=pltpu.CompilerParams(collective_id=0, has_side_effects=True),
    )(jnp.transpose(snapshots, (1, 0, 2)), weights.reshape(1, -1), starts, bins.reshape(1, -1))
    held = [
        pltpu.with_memory_space_constraint(value, pltpu.VMEM)
        for value in (
            rec.reshape(n_freq, per_dev, -1, 2, 128),
            tail.reshape(n_freq, -1, 2, 128),
            energy,
        )
    ]
    modes, energy = pl.pallas_call(
        functools.partial(write_out, (per_dev, n_var, tiles), early),
        out_shape=(
            jax.ShapeDtypeStruct((per_dev * n_var, n_freq, tiles, 2, 128), jnp.float32),
            jax.ShapeDtypeStruct((per_dev,), jnp.float32),
        ),
        in_specs=[vmem] * 3,
        out_specs=(anywhere, vmem),
        scratch_shapes=[dma((2 * per_dev * n_var,))],
    )(*held)
    modes = modes.reshape(per_dev, n_var, n_freq * tiles, 2, 128)
    modes = jnp.transpose(modes, (0, 3, 1, 2, 4)).reshape(
        per_dev, 2, n_var, n_freq * n_local
    )
    return modes, energy


def solution(mesh):
    n_freq, n_pts = mesh.shape["freq"], mesh.shape["pts"]
    return jax.shard_map(
        functools.partial(body, n_freq, n_pts, LENGTH_Z),
        mesh=mesh,
        in_specs=(P(None, None, ("pts", "freq")), P(("pts", "freq")), P(), P()),
        out_specs=(P("freq", None, None, "pts"), P("freq")),
        check_vma=False,
    )
```

time: 38.5 us -> 35.5 us (0.922)
  Pallas kernels: 37.3 us -> 34.7 us
    pallas_call x2, Pallas kernels: 37.3 us -> 34.7 us  [the longest x1 33.2 us: body(): pl.pallas_call(functools.partial(kernel, sizes, split_sizes, early), out_...]
where the time goes in v4:
time: 35.5 us; the launch traced here: 35.4 us
  Pallas kernels  34.7 us (98%)
  between operations  0.64 us (2%)
    pallas_call x1, Pallas kernels, body(): pl.pallas_call(functools.partial(kernel, sizes, split_sizes, early), out_...  33.2 us
    pallas_call x1, Pallas kernels, body(): pl.pallas_call(functools.partial(write_out, (per_dev, n_var, tiles), earl...  1.51 us

profile of v4, /device:TPU:32, one launch (start us, length us, event | category | flops | bytes accessed | tf_op | source)
XLA Modules:
  0.0 35.4 jit_solution(16014778696134486608)
XLA Ops:
  0.6 33.2 %shard_map.59 = (f32[1024,128]{1,0:T(8,128)S(1)}, f32[256,128]{1,0:T(8,128)S(1)}, f32[1,128]{1,0:T(1,128)S(1)}) custom-call(f32[5,256,256]{2,1,0:T(8,128)} %bitcast.12, f32[1,256]{1,0:T(1,128)} %bitcast.13, s32[3]{0:T(128)} %starts_in.1, s32[1,64]{1,0:T(1,128)} %bitcast.14), custom_call_target="tpu_custom_call" | custom-call | tf_op jit(solution)/shard_map/pallas_call | solution.py:442
  33.8 1.5 %shard_map.60 = (f32[10,32,2,2,128]{4,3,2,1,0:T(2,128)}, f32[2]{0:T(128)}) custom-call(f32[32,2,8,2,128]{4,3,2,1,0:T(2,128)S(1)} %bitcast.10, f32[32,4,2,128]{3,2,1,0:T(2,128)S(1)} %bitcast.11, f32[1,128]{1,0:T(1,128)S(1)} %get-tuple-element.9.row), custom_call_target="tpu_custom_call" | custom-call | tf_op jit(solution)/shard_map/pallas_call | solution.py:483

commit v5 on v4

--- a/solution.py
+++ b/solution.py
@@ -1,4 +1,5 @@
 import functools
+import itertools
 import math
 
 import jax
@@ -12,6 +13,7 @@
 NB = 3
 ITERS = 8
 LENGTH_Z = 8
+FAR_FIRST = (4, 3, 5, 2, 6, 1, 7, 0)
 HALF = 64
 PAIRS = ((0, 1), (0, 2), (1, 2))
 MESH = pl.DeviceIdType.MESH
@@ -114,16 +116,16 @@
     steps = [(i, j) for i in range(nx) for j in range(ny) if i or j]
     steps.sort(key=lambda s: -far(s[0], nx) - far(s[1], ny))
     plane = [
-        ({"freq": lax.rem(x + i, nx) * nz + z, "pts": lax.rem(y + j, ny) * 2 + core}, 0 if j else i)
+        ({"freq": lax.rem(x + i, nx) * nz + z, "pts": lax.rem(y + j, ny) * 2 + core}, 0)
         for i, j in steps
     ]
     steps = [(i, j) for i in range(nz) for j in range(2) if i or j]
     steps.sort(key=lambda s: -far(s[0], nz) - 0.5 * s[1])
     line = [
-        ({"freq": x * nz + lax.rem(z + i, nz), "pts": y * 2 + lax.rem(core + j, 2)}, 0)
+        ({"freq": x * nz + lax.rem(z + i, nz), "pts": y * 2 + lax.rem(core + j, 2)}, 0 if j else i)
         for i, j in steps
     ]
-    return (x * ny + y, plane), (z * 2 + core, line)
+    return (z * 2 + core, line), (x * ny + y, plane)
 
 
 def leading(total):
@@ -191,7 +193,7 @@
 
     barrier = pltpu.get_barrier_semaphore()
     near_group, far_group = groups_of(split_sizes)
-    everyone = far_group[1] + near_group[1]
+    everyone = [p for pair in itertools.zip_longest(far_group[1], near_group[1]) for p in pair if p]
     for peer, _ in everyone:
         pl.semaphore_signal(barrier, inc=1, device_id=peer, device_id_type=MESH)
 
@@ -282,24 +284,27 @@
 
     x, z = me_f // nz, lax.rem(me_f, nz)
 
-    def send_ahead(dx):
-        for dz in range(nz):
-            if dx or dz:
-                dest = lax.rem(x + dx, nx) * nz + lax.rem(z + dz, nz)
-                lead(dest, me_f).start()
+    def send_ahead(dz, steps):
+        for dx in steps:
+            dest = lax.rem(x + dx, nx) * nz + lax.rem(z + dz, nz)
+            lead(dest, me_f).start()
 
     pl.semaphore_wait(barrier, len(everyone))
     start_near(mine[:5])
-    send_ahead(0)
-    order = sorted(range(1, nx), key=lambda d: min(d, nx - d))
-    for n, dx in enumerate(order):
-        one_near(nx - dx)
-        if n < 1:
-            send_ahead(dx)
+    order = sorted(range(1, nz), key=lambda d: min(d, nz - d))
+    for dz in reversed(order):
+        send_ahead(dz, (0,))
+    others = range(1, nx)
+    for dz in order[:4]:
+        one_near(nz - dz)
+        send_ahead(dz, others)
+    for dz in order[4:]:
+        one_near(nz - dz)
     near = finish_near()
     start_far(near)
-    for dx in order[1:]:
-        send_ahead(dx)
+    for dz in reversed(order[4:]):
+        send_ahead(dz, others)
+    send_ahead(0, others)
     total = finish_far()
     total = total / float(n_freq * n_pts * n_local * n_var)
 
@@ -396,7 +401,7 @@
     drain_far()
 
 
-def write_out(sizes, early, rec, tail, row, modes, energy, sems):
+def write_out(sizes, early, rec, tail, row, modes, energy, held_energy, sems, sem):
     per_dev, n_var, tiles = sizes
     left = n_var * tiles - early
     copies = []
@@ -418,11 +423,14 @@
                     tail.at[:, pl.ds(kk * early, tiles - cut)],
                     held.at[:, pl.ds(cut, tiles - cut)],
                 )
+    held_energy[...] = row[0, :per_dev]
+    last = pltpu.make_async_copy(held_energy, energy, sem)
+    last.start()
     for copy in copies:
         copy.start()
-    energy[...] = row[0, :per_dev]
     for copy in copies:
         copy.wait()
+    last.wait()
 
 
 def body(n_freq, n_pts, nz, snapshots, weights, starts, bins):
@@ -436,7 +444,7 @@
     tail_rows = max(kf * early * 2, n_freq * 2)
     sizes = (n_freq, n_pts, kf, n_var, n_time, n_local)
     split_sizes = (n_freq // nz, nz, n_pts // 2)
-    near, far = split_sizes[0] * split_sizes[2], 2 * nz
+    near, far = 2 * nz, split_sizes[0] * split_sizes[2]
     vmem, anywhere = (pl.BlockSpec(memory_space=m) for m in (pltpu.VMEM, pl.ANY))
     dma = pltpu.SemaphoreType.DMA
     rec, tail, energy = pl.pallas_call(
@@ -468,7 +476,7 @@
             dma((n_var,)),
             dma((3,)),
         ]
-        + [dma(()), dma((split_sizes[0],)), dma(()), dma((1,))]
+        + [dma(()), dma((nz,)), dma(()), dma((1,))]
         + [dma(())] * 4,
         compiler_params=pltpu.CompilerParams(collective_id=0, has_side_effects=True),
     )(jnp.transpose(snapshots, (1, 0, 2)), weights.reshape(1, -1), starts, bins.reshape(1, -1))
@@ -487,8 +495,12 @@
             jax.ShapeDtypeStruct((per_dev,), jnp.float32),
         ),
         in_specs=[vmem] * 3,
-        out_specs=(anywhere, vmem),
-        scratch_shapes=[dma((2 * per_dev * n_var,))],
+        out_specs=(anywhere, anywhere),
+        scratch_shapes=[
+            pltpu.VMEM((per_dev,), jnp.float32),
+            dma((2 * per_dev * n_var,)),
+            dma(()),
+        ],
     )(*held)
     modes = modes.reshape(per_dev, n_var, n_freq * tiles, 2, 128)
     modes = jnp.transpose(modes, (0, 3, 1, 2, 4)).reshape(

time: 35.5 us -> 34.9 us (0.983)
  Pallas kernels: 34.7 us -> 33.9 us
    pallas_call x1, Pallas kernels: 1.51 us -> 1.02 us  [body(): pl.pallas_call(functools.partial(write_out, (per_dev, n_var, tiles), earl...]
where the time goes in v5:
time: 34.9 us; the launch traced here: 34.5 us
  Pallas kernels  33.9 us (97%)
  between operations  0.64 us (2%)
    pallas_call x1, Pallas kernels, body(): pl.pallas_call(functools.partial(kernel, sizes, split_sizes, early), out_...  32.9 us
    pallas_call x1, Pallas kernels, body(): pl.pallas_call(functools.partial(write_out, (per_dev, n_var, tiles), earl...  1.02 us

profile of v5, /device:TPU:32, one launch (start us, length us, event | category | flops | bytes accessed | tf_op | source)
XLA Modules:
  0.0 34.5 jit_solution(12335096124428962985)
XLA Ops:
  0.6 32.9 %shard_map.59 = (f32[1024,128]{1,0:T(8,128)S(1)}, f32[256,128]{1,0:T(8,128)S(1)}, f32[1,128]{1,0:T(1,128)S(1)}) custom-call(f32[5,256,256]{2,1,0:T(8,128)} %bitcast.12, f32[1,256]{1,0:T(1,128)} %bitcast.13, s32[3]{0:T(128)} %starts_in.1, s32[1,64]{1,0:T(1,128)} %bitcast.14), custom_call_target="tpu_custom_call" | custom-call | tf_op jit(solution)/shard_map/pallas_call | solution.py:450
  33.5 1.0 %shard_map.60 = (f32[10,32,2,2,128]{4,3,2,1,0:T(2,128)}, f32[2]{0:T(128)}) custom-call(f32[32,2,8,2,128]{4,3,2,1,0:T(2,128)S(1)} %bitcast.10, f32[32,4,2,128]{3,2,1,0:T(2,128)S(1)} %bitcast.11, f32[1,128]{1,0:T(1,128)S(1)} %get-tuple-element.9.row), custom_call_target="tpu_custom_call" | custom-call | tf_op jit(solution)/shard_map/pallas_call | solution.py:491

commit v6 on v5

--- a/solution.py
+++ b/solution.py
@@ -295,14 +295,14 @@
     for dz in reversed(order):
         send_ahead(dz, (0,))
     others = range(1, nx)
-    for dz in order[:4]:
+    for dz in order[:2]:
         one_near(nz - dz)
         send_ahead(dz, others)
-    for dz in order[4:]:
+    for dz in order[2:]:
         one_near(nz - dz)
     near = finish_near()
     start_far(near)
-    for dz in reversed(order[4:]):
+    for dz in reversed(order[2:]):
         send_ahead(dz, others)
     send_ahead(0, others)
     total = finish_far()

time: 34.9 us -> 34.6 us (level)
  no operation moved by 1% of the time
where the time goes in v6:
time: 34.6 us; the launch traced here: 34.5 us
  Pallas kernels  33.9 us (98%)
  between operations  0.64 us (2%)
    pallas_call x1, Pallas kernels, body(): pl.pallas_call(functools.partial(kernel, sizes, split_sizes, early), out_...  32.9 us
    pallas_call x1, Pallas kernels, body(): pl.pallas_call(functools.partial(write_out, (per_dev, n_var, tiles), earl...  1.02 us

profile of v6, /device:TPU:32, one launch (start us, length us, event | category | flops | bytes accessed | tf_op | source)
XLA Modules:
  0.0 34.5 jit_solution(5078448993748206860)
XLA Ops:
  0.6 32.9 %shard_map.59 = (f32[1024,128]{1,0:T(8,128)S(1)}, f32[256,128]{1,0:T(8,128)S(1)}, f32[1,128]{1,0:T(1,128)S(1)}) custom-call(f32[5,256,256]{2,1,0:T(8,128)} %bitcast.12, f32[1,256]{1,0:T(1,128)} %bitcast.13, s32[3]{0:T(128)} %starts_in.1, s32[1,64]{1,0:T(1,128)} %bitcast.14), custom_call_target="tpu_custom_call" | custom-call | tf_op jit(solution)/shard_map/pallas_call | solution.py:450
  33.5 1.0 %shard_map.60 = (f32[10,32,2,2,128]{4,3,2,1,0:T(2,128)}, f32[2]{0:T(128)}) custom-call(f32[32,2,8,2,128]{4,3,2,1,0:T(2,128)S(1)} %bitcast.10, f32[32,4,2,128]{3,2,1,0:T(2,128)S(1)} %bitcast.11, f32[1,128]{1,0:T(1,128)S(1)} %get-tuple-element.9.row), custom_call_target="tpu_custom_call" | custom-call | tf_op jit(solution)/shard_map/pallas_call | solution.py:491

commit v7 on v6

--- a/solution.py
+++ b/solution.py
@@ -277,6 +277,8 @@
                         ahead[pl.ds(at, wide, stride=pitch), :] = s[b][part]
         return carry
 
+    pl.semaphore_wait(barrier, len(everyone))
+    start_near(mine[:5])
     if early:
         lax.fori_loop(0, n_oct, pack, 0)
         mine_rows = pl.ds(me_f * pitch, pitch)
@@ -289,8 +291,6 @@
             dest = lax.rem(x + dx, nx) * nz + lax.rem(z + dz, nz)
             lead(dest, me_f).start()
 
-    pl.semaphore_wait(barrier, len(everyone))
-    start_near(mine[:5])
     order = sorted(range(1, nz), key=lambda d: min(d, nz - d))
     for dz in reversed(order):
         send_ahead(dz, (0,))

time: 34.6 us -> 34.6 us (level)
  no operation moved by 1% of the time
where the time goes in v7:
time: 34.6 us; the launch traced here: 34.5 us
  Pallas kernels  33.8 us (98%)
  between operations  0.64 us (2%)
    pallas_call x1, Pallas kernels, body(): pl.pallas_call(functools.partial(kernel, sizes, split_sizes, early), out_...  32.8 us
    pallas_call x1, Pallas kernels, body(): pl.pallas_call(functools.partial(write_out, (per_dev, n_var, tiles), earl...  1.02 us

profile of v7, /device:TPU:32, one launch (start us, length us, event | category | flops | bytes accessed | tf_op | source)
XLA Modules:
  0.0 34.5 jit_solution(3853078194523940418)
XLA Ops:
  0.6 32.8 %shard_map.59 = (f32[1024,128]{1,0:T(8,128)S(1)}, f32[256,128]{1,0:T(8,128)S(1)}, f32[1,128]{1,0:T(1,128)S(1)}) custom-call(f32[5,256,256]{2,1,0:T(8,128)} %bitcast.12, f32[1,256]{1,0:T(1,128)} %bitcast.13, s32[3]{0:T(128)} %starts_in.1, s32[1,64]{1,0:T(1,128)} %bitcast.14), custom_call_target="tpu_custom_call" | custom-call | tf_op jit(solution)/shard_map/pallas_call | solution.py:450
  33.4 1.0 %shard_map.60 = (f32[10,32,2,2,128]{4,3,2,1,0:T(2,128)}, f32[2]{0:T(128)}) custom-call(f32[32,2,8,2,128]{4,3,2,1,0:T(2,128)S(1)} %bitcast.10, f32[32,4,2,128]{3,2,1,0:T(2,128)S(1)} %bitcast.11, f32[1,128]{1,0:T(1,128)S(1)} %get-tuple-element.9.row), custom_call_target="tpu_custom_call" | custom-call | tf_op jit(solution)/shard_map/pallas_call | solution.py:491
